TPU v7x, 32 devices: a whole 2x2x4 slice. The times are simulated.
32 devices in a mesh: sub: 16 (over z, y, x), agg: 2 (over core).
Axes of the slice: x: 2, y: 2, z: 4, core: 2. Of those that a mesh axis runs over, the one named last changes fastest.
Arguments:
- block_values: float32 [7, 4, 4, 32768], P(None, None, None, ('sub', 'agg'))
- block_cols: int32 [7, 32768], P(None, ('sub', 'agg')), may hold values from 0 to 32767, as said below
- coarse_rhs: float32 [4, 32768], P(None, ('sub', 'agg'))
- guess: float32 [4, 32768], P(None, ('sub', 'agg')), may hold values from -3 to 3
- bound_low: int32 [1], replicated, may hold values from 20 to 26
- bound_high: int32 [1], replicated, may hold values from 32 to 40
Outputs:
- smoothed: float32 [4, 32768], P(None, ('sub', 'agg'))
- residual: float32 [4, 32768], P(None, ('sub', 'agg'))
- residual_rms: float32 [1], replicated
Inputs may be any that keep to these rules, and one draw needn't show every extreme that they name: Block rows form 32768 / 1024 planes of 1024 consecutive rows, in a periodic order. block_cols[0] is the row itself, block_cols[1] a row of the previous plane, block_cols[2] a row of the next plane, block_cols[3] to block_cols[6] rows of the same plane.
All inputs are finite; a program needn't handle non-finite values.
Results may differ from a plain program's by a relative error of at most 0.0001.
Values sent between devices are 32-bit elements; how exact they have to be, the bound alone decides.
A program may use at most 64 MiB of HBM per device.

v0:
```python
import functools

import jax
import jax.numpy as jnp
from jax import lax
from jax.experimental import pallas as pl
from jax.experimental.pallas import tpu as pltpu
from jax.sharding import PartitionSpec as P

STEPS = 4
LANES = 128
MESH = pl.DeviceIdType.MESH


def group_size(devices):
    size = 1
    while size * size < devices or devices % size:
        size += 1
    return size


def gather_lanes(rows, index):
    return jnp.take_along_axis(rows, index, axis=1, mode="promise_in_bounds")


def kernel(
    subs, aggs, shape,
    values_hbm, cols_hbm, rhs_hbm, guess_hbm, low_ref, high_ref,
    smoothed_hbm, residual_hbm, rms_ref,
    values, cols, cols_flat, rhs, field, beside, lane_of, tile_of, coef,
    smoothed_out, residual_out, near_sums, far_sums,
    values_sem, load_sem, store_sem, send_sem, recv_sem,
    near_send, near_recv, far_send, far_recv,
):
    blocks, comp, tiles = shape
    devices = subs * aggs
    rows = tiles * LANES
    me = lax.axis_index("sub") * aggs + lax.axis_index("agg")

    def coords(device):
        return (device // aggs, device % aggs)

    following = lax.rem(me + 1, devices)
    previous = lax.rem(me + devices - 1, devices)
    near = group_size(devices)
    far = devices // near
    near_me = lax.rem(me, near)
    near_base = me - near_me
    far_me = me // near
    near_partners = [near_base + lax.rem(near_me + d, near) for d in range(1, near)]
    far_partners = [lax.rem(me + d * near, devices) for d in range(1, far)]

    barrier = pltpu.get_barrier_semaphore()
    partners = [following, previous] + far_partners + near_partners
    for partner in partners:
        pl.semaphore_signal(barrier, inc=1, device_id=coords(partner), device_id_type=MESH)

    load_cols = pltpu.make_async_copy(cols_hbm, cols, load_sem.at[0])
    load_guess = pltpu.make_async_copy(guess_hbm, field.at[0], load_sem.at[1])
    load_rhs = pltpu.make_async_copy(rhs_hbm, rhs, load_sem.at[2])
    load_cols.start()
    load_guess.start()
    own = [0] + list(range(3, blocks))
    per_block = comp * comp * tiles

    def load_values(k):
        part = pl.ds(k * per_block, per_block)
        return pltpu.make_async_copy(values_hbm.at[part], values.at[part], values_sem.at[k])

    for k in own + [1, 2]:
        load_values(k).start()
    load_rhs.start()

    pl.semaphore_wait(barrier, len(partners))

    def send(step, source, way):
        return pltpu.make_async_remote_copy(
            src_ref=source,
            dst_ref=beside.at[step, way],
            send_sem=send_sem.at[step, way],
            recv_sem=recv_sem.at[step, way],
            device_id=coords(following if way == 0 else previous),
            device_id_type=MESH,
        )

    for way in range(2):
        send(0, guess_hbm, way).start()

    low = jnp.full((tiles, LANES), low_ref[0], jnp.int32).astype(jnp.float32) / 4.0
    high = jnp.full((tiles, LANES), high_ref[0], jnp.int32).astype(jnp.float32) / 4.0
    centre = (high + low) / 2.0
    half = (high - low) / 2.0
    spread = centre / half
    ratio = 1.0 / spread
    coef[0, 0] = jnp.zeros((tiles, LANES), jnp.float32)
    coef[0, 1] = 1.0 / centre
    for t in range(1, STEPS):
        ahead = 1.0 / (2.0 * spread - ratio)
        coef[t, 0] = ahead * ratio
        coef[t, 1] = 2.0 * ahead / half
        ratio = ahead

    load_cols.wait()
    for c in range(tiles):
        cols_flat[pl.ds(c * 8, blocks), :] = cols[:, c * LANES:(c + 1) * LANES]
    for k in range(1, blocks):
        plane = {1: previous, 2: following}.get(k, me)
        local = cols_flat[pl.ds(k, tiles, stride=8), :] - plane * rows
        lane_of[k] = local & (LANES - 1)
        tile_of[k] = local >> 7

    def taken(source, k):
        lanes, tile = lane_of[k], tile_of[k]
        out = [None] * comp
        for r in range(tiles):
            here = tile == r
            for j in range(comp):
                row = jnp.broadcast_to(source[pl.ds(r * comp + j, 1), :], (tiles, LANES))
                got = gather_lanes(row, lanes)
                out[j] = got if r == 0 else jnp.where(here, got, out[j])
        return out

    def combine(k, got, total):
        total = list(total)
        for i in range(comp):
            base = (k * comp + i) * comp * tiles
            for j in range(comp):
                total[i] = total[i] - values[pl.ds(base + j, tiles, stride=comp), :] * got[j]
        return total

    def own_part(t, residual):
        source = field.at[t]
        direct = [source[pl.ds(j, tiles, stride=comp), :] for j in range(comp)]
        residual = combine(0, direct, residual)
        for k in own[1:]:
            residual = combine(k, taken(source, k), residual)
        return direct, residual

    def far_part(t, residual):
        for way in range(2):
            send(t, field.at[t], way).wait_recv()
            residual = combine(1 + way, taken(beside.at[t, way], 1 + way), residual)
        return residual

    load_guess.wait()
    load_rhs.wait()
    for k in own + [1, 2]:
        load_values(k).wait()

    def step(t, carry):
        smoothed, residual = carry
        direct, residual = own_part(t, residual)
        smoothed = [s + d for s, d in zip(smoothed, direct)]
        residual = far_part(t, residual)
        for j in range(comp):
            field[t + 1, pl.ds(j, tiles, stride=comp), :] = (
                coef[t, 0] * direct[j] + coef[t, 1] * residual[j]
            )
        for way in range(2):
            send(t + 1, field.at[t + 1], way).start()
        return smoothed, residual

    smoothed = [jnp.zeros((tiles, LANES), jnp.float32) for j in range(comp)]
    residual = [rhs[pl.ds(j, tiles, stride=comp), :] for j in range(comp)]
    smoothed, residual = lax.fori_loop(0, STEPS, step, (smoothed, residual))

    direct, residual = own_part(STEPS, residual)
    for j in range(comp):
        smoothed_out[pl.ds(j, tiles, stride=comp), :] = smoothed[j] + direct[j]
    store_smoothed = pltpu.make_async_copy(smoothed_out, smoothed_hbm, store_sem.at[0])
    store_smoothed.start()
    residual = far_part(STEPS, residual)

    squares = residual[0] * residual[0]
    for j in range(1, comp):
        squares = squares + residual[j] * residual[j]
    partial = jnp.sum(squares, axis=0, keepdims=True)

    def spread_sums(sums, slot, partner, send_sems, recv_sems, d):
        return pltpu.make_async_remote_copy(
            src_ref=sums.at[slot],
            dst_ref=sums.at[slot],
            send_sem=send_sems.at[d],
            recv_sem=recv_sems.at[slot],
            device_id=coords(partner),
            device_id_type=MESH,
        )

    def total_over(partial, sums, size, place, partners, send_sems, recv_sems):
        sums[place] = partial
        for d, partner in enumerate(partners):
            spread_sums(sums, place, partner, send_sems, recv_sems, d).start()

        def finish():
            for d, partner in enumerate(partners):
                slot = lax.rem(place + d + 1, size)
                spread_sums(sums, slot, partner, send_sems, recv_sems, d).wait_recv()
            total = sums[0]
            for slot in range(1, size):
                total = total + sums[slot]
            return total

        return finish

    finish = total_over(partial, near_sums, near, near_me, near_partners, near_send, near_recv)
    for j in range(comp):
        residual_out[pl.ds(j, tiles, stride=comp), :] = residual[j]
    store_residual = pltpu.make_async_copy(residual_out, residual_hbm, store_sem.at[1])
    store_residual.start()
    partial = finish()
    finish = total_over(partial, far_sums, far, far_me, far_partners, far_send, far_recv)
    total = finish()
    count = float(comp * rows * devices)
    rms = jnp.sqrt(jnp.sum(total, axis=1, keepdims=True) / count + 1e-06)
    rms_ref[0] = rms[0, 0]

    for t in range(STEPS + 1):
        for way in range(2):
            send(t, field.at[t], way).wait_send()
    for d, partner in enumerate(near_partners):
        spread_sums(near_sums, near_me, partner, near_send, near_recv, d).wait_send()
    for d, partner in enumerate(far_partners):
        spread_sums(far_sums, far_me, partner, far_send, far_recv, d).wait_send()
    store_smoothed.wait()
    store_residual.wait()


def flat(field, tiles):
    comp = field.shape[-2]
    lead = field.shape[:-2]
    cut = field.reshape(lead + (comp, tiles, LANES))
    return jnp.swapaxes(cut, -3, -2).reshape(-1, LANES)


def unflat(field, comp):
    tiles = field.shape[0] // comp
    return jnp.swapaxes(field.reshape(tiles, comp, LANES), 0, 1).reshape(comp, tiles * LANES)


def shards(subs, aggs, block_values, block_cols, coarse_rhs, guess, bound_low, bound_high):
    blocks, comp, _, rows = block_values.shape
    tiles = rows // LANES
    devices = subs * aggs
    near = group_size(devices)
    far = devices // near
    f32 = jnp.float32
    plane = (tiles * comp, LANES)
    anywhere = pl.BlockSpec(memory_space=pl.ANY)
    scalar = pl.BlockSpec(memory_space=pltpu.SMEM)
    dma = pltpu.SemaphoreType.DMA
    smoothed, residual, rms = pl.pallas_call(
        functools.partial(kernel, subs, aggs, (blocks, comp, tiles)),
        out_shape=(
            jax.ShapeDtypeStruct(plane, f32),
            jax.ShapeDtypeStruct(plane, f32),
            jax.ShapeDtypeStruct((1,), f32),
        ),
        in_specs=[anywhere] * 4 + [scalar] * 2,
        out_specs=(anywhere, anywhere, scalar),
        scratch_shapes=[
            pltpu.VMEM((blocks * comp * comp * tiles, LANES), f32),
            pltpu.VMEM((blocks, rows), jnp.int32),
            pltpu.VMEM((8 * tiles, LANES), jnp.int32),
            pltpu.VMEM(plane, f32),
            pltpu.VMEM((STEPS + 1,) + plane, f32),
            pltpu.VMEM((STEPS + 1, 2) + plane, f32),
            pltpu.VMEM((blocks, tiles, LANES), jnp.int32),
            pltpu.VMEM((blocks, tiles, LANES), jnp.int32),
            pltpu.VMEM((STEPS, 2, tiles, LANES), f32),
            pltpu.VMEM(plane, f32),
            pltpu.VMEM(plane, f32),
            pltpu.VMEM((near, 1, LANES), f32),
            pltpu.VMEM((far, 1, LANES), f32),
            dma((blocks,)),
            dma((3,)),
            dma((2,)),
            dma((STEPS + 1, 2)),
            dma((STEPS + 1, 2)),
            dma((max(near - 1, 1),)),
            dma((near,)),
            dma((max(far - 1, 1),)),
            dma((far,)),
        ],
        compiler_params=pltpu.CompilerParams(collective_id=0, has_side_effects=True),
    )(
        flat(block_values, tiles), block_cols, flat(coarse_rhs, tiles), flat(guess, tiles),
        bound_low, bound_high,
    )
    return unflat(smoothed, comp), unflat(residual, comp), rms


def solution(mesh):
    split = ("sub", "agg")
    return jax.shard_map(
        functools.partial(shards, mesh.shape["sub"], mesh.shape["agg"]),
        mesh=mesh,
        in_specs=(
            P(None, None, None, split),
            P(None, split),
            P(None, split),
            P(None, split),
            P(),
            P(),
        ),
        out_specs=(P(None, split), P(None, split), P()),
        check_vma=False,
    )
```

profile of v0, /device:TPU:0, one launch (start us, length us, event | category | flops | bytes accessed | tf_op | source)
XLA Modules:
  0.0 40.7 jit_solution(18395555619956010)
XLA Ops:
  1.9 35.1 %shard_map.85 = (f32[32,128]{1,0:T(8,128)}, f32[32,128]{1,0:T(8,128)}, f32[1]{0:T(128)}) custom-call(f32[896,128]{1,0:T(8,128)} %bitcast.25, s32[7,1024]{1,0:T(8,128)} %cols_hbm.1, f32[32,128]{1,0:T(8,128)} %bitcast.26, f32[32,128]{1,0:T(8,128)} %bitcast.27, s32[1]{0:T(128)S(6)} %copy.17.low_ref, s32[1]{0:T(128)S(6)} %copy.18.high_ref), custom_call_target="tpu_custom_call" | custom-call | tf_op jit(solution)/shard_map/pallas_call | solution.py:251
  37.0 0.0 copy-start
  37.0 1.3 %copy.19 = f32[4,1024]{1,0:T(4,128)} copy(f32[4,1024]{1,0:T(4,128)} %bitcast.29) | data formatting | bytes 32768
  38.3 0.0 copy-done
  38.3 0.6 %copy.20 = f32[4,1024]{1,0:T(4,128)} copy(f32[4,1024]{1,0:T(4,128)S(1)} %bitcast.28) | data formatting | bytes 32768
Async XLA Ops:
  37.0 1.3 %copy-start = (f32[32,128]{1,0:T(8,128)S(1)}, f32[32,128]{1,0:T(8,128)}, u32[]{:S(2)}) copy-start(f32[32,128]{1,0:T(8,128)} %get-tuple-element.7) | copy-start | bytes 49156
where the time goes:
time: 41 us; the launch traced here: 40.7 us
  Pallas kernels  35.1 us (86%)
  between operations  3.68 us (9%)
  local copies, waits for them, and re-layouts  1.94 us (5%)
    pallas_call x1, Pallas kernels, shards(): pl.pallas_call(functools.partial(kernel, subs, aggs, (blocks, comp, tiles...  35.1 us
    unnamed x4, local copies, waits for them, and re-layouts  1.94 us

commit v1 on v0

--- a/solution.py
+++ b/solution.py
@@ -8,11 +8,14 @@
 from jax.sharding import PartitionSpec as P
 
 STEPS = 4
+ONE_ROUND = 32
 LANES = 128
 MESH = pl.DeviceIdType.MESH
 
 
 def group_size(devices):
+    if devices <= ONE_ROUND:
+        return devices
     size = 1
     while size * size < devices or devices % size:
         size += 1
@@ -25,9 +28,9 @@
 
 def kernel(
     subs, aggs, shape,
-    values_hbm, cols_hbm, rhs_hbm, guess_hbm, low_ref, high_ref,
+    values_hbm, cols_hbm, rhs_hbm, guess_hbm, low_hbm, high_hbm,
     smoothed_hbm, residual_hbm, rms_ref,
-    values, cols, cols_flat, rhs, field, beside, lane_of, tile_of, coef,
+    low_ref, high_ref, values, cols, cols_flat, rhs, field, beside, lane_of, tile_of, coef,
     smoothed_out, residual_out, near_sums, far_sums,
     values_sem, load_sem, store_sem, send_sem, recv_sem,
     near_send, near_recv, far_send, far_recv,
@@ -58,8 +61,10 @@
     load_cols = pltpu.make_async_copy(cols_hbm, cols, load_sem.at[0])
     load_guess = pltpu.make_async_copy(guess_hbm, field.at[0], load_sem.at[1])
     load_rhs = pltpu.make_async_copy(rhs_hbm, rhs, load_sem.at[2])
-    load_cols.start()
-    load_guess.start()
+    load_low = pltpu.make_async_copy(low_hbm, low_ref, load_sem.at[3])
+    load_high = pltpu.make_async_copy(high_hbm, high_ref, load_sem.at[4])
+    for load in (load_guess, load_cols, load_low, load_high):
+        load.start()
     own = [0] + list(range(3, blocks))
     per_block = comp * comp * tiles
 
@@ -71,6 +76,7 @@
         load_values(k).start()
     load_rhs.start()
 
+    load_guess.wait()
     pl.semaphore_wait(barrier, len(partners))
 
     def send(step, source, way):
@@ -79,13 +85,15 @@
             dst_ref=beside.at[step, way],
             send_sem=send_sem.at[step, way],
             recv_sem=recv_sem.at[step, way],
-            device_id=coords(following if way == 0 else previous),
+            device_id=coords(lax.rem(me + 1 + way * (devices - 2), devices)),
             device_id_type=MESH,
         )
 
     for way in range(2):
-        send(0, guess_hbm, way).start()
-
+        send(0, field.at[0], way).start()
+
+    load_low.wait()
+    load_high.wait()
     low = jnp.full((tiles, LANES), low_ref[0], jnp.int32).astype(jnp.float32) / 4.0
     high = jnp.full((tiles, LANES), high_ref[0], jnp.int32).astype(jnp.float32) / 4.0
     centre = (high + low) / 2.0
@@ -137,12 +145,12 @@
         return direct, residual
 
     def far_part(t, residual):
-        for way in range(2):
+        even = 1 - lax.rem(me, 2)
+        for way in (even, 1 - even):
             send(t, field.at[t], way).wait_recv()
             residual = combine(1 + way, taken(beside.at[t, way], 1 + way), residual)
         return residual
 
-    load_guess.wait()
     load_rhs.wait()
     for k in own + [1, 2]:
         load_values(k).wait()
@@ -207,9 +215,9 @@
         residual_out[pl.ds(j, tiles, stride=comp), :] = residual[j]
     store_residual = pltpu.make_async_copy(residual_out, residual_hbm, store_sem.at[1])
     store_residual.start()
-    partial = finish()
-    finish = total_over(partial, far_sums, far, far_me, far_partners, far_send, far_recv)
     total = finish()
+    if far > 1:
+        total = total_over(total, far_sums, far, far_me, far_partners, far_send, far_recv)()
     count = float(comp * rows * devices)
     rms = jnp.sqrt(jnp.sum(total, axis=1, keepdims=True) / count + 1e-06)
     rms_ref[0] = rms[0, 0]
@@ -246,6 +254,7 @@
     f32 = jnp.float32
     plane = (tiles * comp, LANES)
     anywhere = pl.BlockSpec(memory_space=pl.ANY)
+    in_hbm = pl.BlockSpec(memory_space=pltpu.HBM)
     scalar = pl.BlockSpec(memory_space=pltpu.SMEM)
     dma = pltpu.SemaphoreType.DMA
     smoothed, residual, rms = pl.pallas_call(
@@ -255,9 +264,11 @@
             jax.ShapeDtypeStruct(plane, f32),
             jax.ShapeDtypeStruct((1,), f32),
         ),
-        in_specs=[anywhere] * 4 + [scalar] * 2,
+        in_specs=[in_hbm] * 6,
         out_specs=(anywhere, anywhere, scalar),
         scratch_shapes=[
+            pltpu.SMEM((1,), jnp.int32),
+            pltpu.SMEM((1,), jnp.int32),
             pltpu.VMEM((blocks * comp * comp * tiles, LANES), f32),
             pltpu.VMEM((blocks, rows), jnp.int32),
             pltpu.VMEM((8 * tiles, LANES), jnp.int32),
@@ -272,7 +283,7 @@
             pltpu.VMEM((near, 1, LANES), f32),
             pltpu.VMEM((far, 1, LANES), f32),
             dma((blocks,)),
-            dma((3,)),
+            dma((5,)),
             dma((2,)),
             dma((STEPS + 1, 2)),
             dma((STEPS + 1, 2)),

time: 41 us -> 39.6 us (0.966)
  Pallas kernels: 35.1 us -> 33.7 us
    pallas_call x1, Pallas kernels: 35.1 us -> 33.7 us  [shards(): pl.pallas_call(functools.partial(kernel, subs, aggs, (blocks, comp, tiles...]
where the time goes in v1:
time: 39.6 us; the launch traced here: 39.3 us
  Pallas kernels  33.7 us (85%)
  between operations  3.68 us (9%)
  local copies, waits for them, and re-layouts  1.94 us (5%)
    pallas_call x1, Pallas kernels, shards(): pl.pallas_call(functools.partial(kernel, subs, aggs, (blocks, comp, tiles...  33.7 us
    unnamed x4, local copies, waits for them, and re-layouts  1.94 us

profile of v1, /device:TPU:0, one launch (start us, length us, event | category | flops | bytes accessed | tf_op | source)
XLA Modules:
  0.0 39.3 jit_solution(9604209027315709340)
XLA Ops:
  1.9 33.7 %shard_map.85 = (f32[32,128]{1,0:T(8,128)}, f32[32,128]{1,0:T(8,128)}, f32[1]{0:T(128)}) custom-call(f32[896,128]{1,0:T(8,128)} %bitcast.25, s32[7,1024]{1,0:T(8,128)} %cols_hbm.1, f32[32,128]{1,0:T(8,128)} %bitcast.26, f32[32,128]{1,0:T(8,128)} %bitcast.27, s32[1]{0:T(128)S(6)} %copy.17.low_hbm, s32[1]{0:T(128)S(6)} %copy.18.high_hbm), custom_call_target="tpu_custom_call" | custom-call | tf_op jit(solution)/shard_map/pallas_call | solution.py:260
  35.6 0.0 copy-start
  35.6 1.3 %copy.19 = f32[4,1024]{1,0:T(4,128)} copy(f32[4,1024]{1,0:T(4,128)} %bitcast.29) | data formatting | bytes 32768
  36.9 0.0 copy-done
  36.9 0.6 %copy.20 = f32[4,1024]{1,0:T(4,128)} copy(f32[4,1024]{1,0:T(4,128)S(1)} %bitcast.28) | data formatting | bytes 32768
Async XLA Ops:
  35.6 1.3 %copy-start = (f32[32,128]{1,0:T(8,128)S(1)}, f32[32,128]{1,0:T(8,128)}, u32[]{:S(2)}) copy-start(f32[32,128]{1,0:T(8,128)} %get-tuple-element.7) | copy-start | bytes 49156

commit v2 on v1

--- a/solution.py
+++ b/solution.py
@@ -29,10 +29,10 @@
 def kernel(
     subs, aggs, shape,
     values_hbm, cols_hbm, rhs_hbm, guess_hbm, low_hbm, high_hbm,
-    smoothed_hbm, residual_hbm, rms_ref,
+    smoothed_out, residual_out, rms_ref,
     low_ref, high_ref, values, cols, cols_flat, rhs, field, beside, lane_of, tile_of, coef,
-    smoothed_out, residual_out, near_sums, far_sums,
-    values_sem, load_sem, store_sem, send_sem, recv_sem,
+    near_sums, far_sums,
+    values_sem, load_sem, send_sem, recv_sem,
     near_send, near_recv, far_send, far_recv,
 ):
     blocks, comp, tiles = shape
@@ -175,8 +175,6 @@
     direct, residual = own_part(STEPS, residual)
     for j in range(comp):
         smoothed_out[pl.ds(j, tiles, stride=comp), :] = smoothed[j] + direct[j]
-    store_smoothed = pltpu.make_async_copy(smoothed_out, smoothed_hbm, store_sem.at[0])
-    store_smoothed.start()
     residual = far_part(STEPS, residual)
 
     squares = residual[0] * residual[0]
@@ -213,8 +211,6 @@
     finish = total_over(partial, near_sums, near, near_me, near_partners, near_send, near_recv)
     for j in range(comp):
         residual_out[pl.ds(j, tiles, stride=comp), :] = residual[j]
-    store_residual = pltpu.make_async_copy(residual_out, residual_hbm, store_sem.at[1])
-    store_residual.start()
     total = finish()
     if far > 1:
         total = total_over(total, far_sums, far, far_me, far_partners, far_send, far_recv)()
@@ -229,8 +225,6 @@
         spread_sums(near_sums, near_me, partner, near_send, near_recv, d).wait_send()
     for d, partner in enumerate(far_partners):
         spread_sums(far_sums, far_me, partner, far_send, far_recv, d).wait_send()
-    store_smoothed.wait()
-    store_residual.wait()
 
 
 def flat(field, tiles):
@@ -253,7 +247,7 @@
     far = devices // near
     f32 = jnp.float32
     plane = (tiles * comp, LANES)
-    anywhere = pl.BlockSpec(memory_space=pl.ANY)
+    in_vmem = pl.BlockSpec(memory_space=pltpu.VMEM)
     in_hbm = pl.BlockSpec(memory_space=pltpu.HBM)
     scalar = pl.BlockSpec(memory_space=pltpu.SMEM)
     dma = pltpu.SemaphoreType.DMA
@@ -265,7 +259,7 @@
             jax.ShapeDtypeStruct((1,), f32),
         ),
         in_specs=[in_hbm] * 6,
-        out_specs=(anywhere, anywhere, scalar),
+        out_specs=(in_vmem, in_vmem, scalar),
         scratch_shapes=[
             pltpu.SMEM((1,), jnp.int32),
             pltpu.SMEM((1,), jnp.int32),
@@ -278,13 +272,10 @@
             pltpu.VMEM((blocks, tiles, LANES), jnp.int32),
             pltpu.VMEM((blocks, tiles, LANES), jnp.int32),
             pltpu.VMEM((STEPS, 2, tiles, LANES), f32),
-            pltpu.VMEM(plane, f32),
-            pltpu.VMEM(plane, f32),
             pltpu.VMEM((near, 1, LANES), f32),
             pltpu.VMEM((far, 1, LANES), f32),
             dma((blocks,)),
             dma((5,)),
-            dma((2,)),
             dma((STEPS + 1, 2)),
             dma((STEPS + 1, 2)),
             dma((max(near - 1, 1),)),
@@ -292,9 +283,14 @@
             dma((max(far - 1, 1),)),
             dma((far,)),
         ],
-        compiler_params=pltpu.CompilerParams(collective_id=0, has_side_effects=True),
+        compiler_params=pltpu.CompilerParams(collective_id=0, has_side_effects=True, vmem_limit_bytes=8 * 1024 * 1024),
     )(
-        flat(block_values, tiles), block_cols, flat(coarse_rhs, tiles), flat(guess, tiles),
+        *[
+            pltpu.with_memory_space_constraint(x, pltpu.HBM)
+            for x in (
+                flat(block_values, tiles), block_cols, flat(coarse_rhs, tiles), flat(guess, tiles),
+            )
+        ],
         bound_low, bound_high,
     )
     return unflat(smoothed, comp), unflat(residual, comp), rms

time: 39.6 us -> 38.7 us (0.977)
  local copies, waits for them, and re-layouts: 1.94 us -> 1.21 us
    unnamed x4 -> x2, local copies, waits for them, and re-layouts: 1.94 us -> 1.21 us
where the time goes in v2:
time: 38.7 us; the launch traced here: 38.5 us
  Pallas kernels  33.6 us (87%)
  between operations  3.62 us (9%)
  local copies, waits for them, and re-layouts  1.21 us (3%)
    pallas_call x1, Pallas kernels, shards(): pl.pallas_call(functools.partial(kernel, subs, aggs, (blocks, comp, tiles...  33.6 us
    unnamed x2, local copies, waits for them, and re-layouts  1.21 us

profile of v2, /device:TPU:0, one launch (start us, length us, event | category | flops | bytes accessed | tf_op | source)
XLA Modules:
  0.0 38.5 jit_solution(13017304522094356691)
XLA Ops:
  1.9 33.6 %shard_map.85 = (f32[32,128]{1,0:T(8,128)S(1)}, f32[32,128]{1,0:T(8,128)S(1)}, f32[1]{0:T(128)}) custom-call(f32[896,128]{1,0:T(8,128)} %bitcast.27, s32[7,1024]{1,0:T(8,128)} %cols_hbm.1, f32[32,128]{1,0:T(8,128)} %bitcast.28, f32[32,128]{1,0:T(8,128)} %bitcast.29, s32[1]{0:T(128)S(6)} %copy.17.low_hbm, s32[1]{0:T(128)S(6)} %copy.18.high_hbm), custom_call_target="tpu_custom_call" | custom-call | tf_op jit(solution)/shard_map/pallas_call | solution.py:254
  35.6 0.6 %copy.19 = f32[4,1024]{1,0:T(4,128)} copy(f32[4,1024]{1,0:T(4,128)S(1)} %bitcast.26) | data formatting | bytes 32768
  36.2 0.6 %copy.20 = f32[4,1024]{1,0:T(4,128)} copy(f32[4,1024]{1,0:T(4,128)S(1)} %bitcast.25) | data formatting | bytes 32768

commit v3 on v2

--- a/solution.py
+++ b/solution.py
@@ -13,24 +13,15 @@
 MESH = pl.DeviceIdType.MESH
 
 
-def group_size(devices):
-    if devices <= ONE_ROUND:
-        return devices
-    size = 1
-    while size * size < devices or devices % size:
-        size += 1
-    return size
-
-
 def gather_lanes(rows, index):
     return jnp.take_along_axis(rows, index, axis=1, mode="promise_in_bounds")
 
 
 def kernel(
     subs, aggs, shape,
-    values_hbm, cols_hbm, rhs_hbm, guess_hbm, low_hbm, high_hbm,
+    values_hbm, cols_hbm, rhs_hbm, guess_hbm, low_ref, high_ref,
     smoothed_out, residual_out, rms_ref,
-    low_ref, high_ref, values, cols, cols_flat, rhs, field, beside, lane_of, tile_of, coef,
+    values, cols, cols_flat, rhs, field, beside, lane_of, tile_of, coef,
     near_sums, far_sums,
     values_sem, load_sem, send_sem, recv_sem,
     near_send, near_recv, far_send, far_recv,
@@ -38,32 +29,10 @@
     blocks, comp, tiles = shape
     devices = subs * aggs
     rows = tiles * LANES
-    me = lax.axis_index("sub") * aggs + lax.axis_index("agg")
-
-    def coords(device):
-        return (device // aggs, device % aggs)
-
-    following = lax.rem(me + 1, devices)
-    previous = lax.rem(me + devices - 1, devices)
-    near = group_size(devices)
-    far = devices // near
-    near_me = lax.rem(me, near)
-    near_base = me - near_me
-    far_me = me // near
-    near_partners = [near_base + lax.rem(near_me + d, near) for d in range(1, near)]
-    far_partners = [lax.rem(me + d * near, devices) for d in range(1, far)]
-
-    barrier = pltpu.get_barrier_semaphore()
-    partners = [following, previous] + far_partners + near_partners
-    for partner in partners:
-        pl.semaphore_signal(barrier, inc=1, device_id=coords(partner), device_id_type=MESH)
-
     load_cols = pltpu.make_async_copy(cols_hbm, cols, load_sem.at[0])
     load_guess = pltpu.make_async_copy(guess_hbm, field.at[0], load_sem.at[1])
     load_rhs = pltpu.make_async_copy(rhs_hbm, rhs, load_sem.at[2])
-    load_low = pltpu.make_async_copy(low_hbm, low_ref, load_sem.at[3])
-    load_high = pltpu.make_async_copy(high_hbm, high_ref, load_sem.at[4])
-    for load in (load_guess, load_cols, load_low, load_high):
+    for load in (load_guess, load_cols):
         load.start()
     own = [0] + list(range(3, blocks))
     per_block = comp * comp * tiles
@@ -75,6 +44,44 @@
     for k in own + [1, 2]:
         load_values(k).start()
     load_rhs.start()
+
+    sub, agg = lax.axis_index("sub"), lax.axis_index("agg")
+    me = sub * aggs + agg
+
+    def ahead_of(place, by, size):
+        to = place + by
+        return jnp.where(to >= size, to - size, to)
+
+    def beside_me(by_sub, by_agg):
+        return (ahead_of(sub, by_sub, subs), ahead_of(agg, by_agg, aggs))
+
+    def ring(way):
+        turn = jnp.where(way == 0, agg == aggs - 1, agg == 0)
+        to_sub = jnp.where(way == 0, ahead_of(sub, 1, subs), ahead_of(sub, subs - 1, subs))
+        to_agg = jnp.where(way == 0, ahead_of(agg, 1, aggs), ahead_of(agg, aggs - 1, aggs))
+        return (jnp.where(turn, to_sub, sub), to_agg)
+
+    following = ahead_of(me, 1, devices)
+    previous = ahead_of(me, devices - 1, devices)
+    one_round = devices <= ONE_ROUND
+    if one_round:
+        near_steps = [(a, b) for a in range(subs) for b in range(aggs)][1:]
+        near_steps = near_steps[::-1]
+        near, near_me = devices, me
+        far_steps = []
+    else:
+        near_steps = [(0, b) for b in range(1, aggs)]
+        near, near_me = aggs, agg
+        far_steps = [(a, 0) for a in range(1, subs)]
+    near_partners = [beside_me(a, b) for a, b in near_steps]
+    far_partners = [beside_me(a, b) for a, b in far_steps]
+
+    barrier = pltpu.get_barrier_semaphore()
+    partners = far_partners + near_partners
+    if not one_round:
+        partners = [ring(0), ring(1)] + partners
+    for partner in partners:
+        pl.semaphore_signal(barrier, inc=1, device_id=partner, device_id_type=MESH)
 
     load_guess.wait()
     pl.semaphore_wait(barrier, len(partners))
@@ -85,15 +92,13 @@
             dst_ref=beside.at[step, way],
             send_sem=send_sem.at[step, way],
             recv_sem=recv_sem.at[step, way],
-            device_id=coords(lax.rem(me + 1 + way * (devices - 2), devices)),
+            device_id=ring(way),
             device_id_type=MESH,
         )
 
     for way in range(2):
         send(0, field.at[0], way).start()
 
-    load_low.wait()
-    load_high.wait()
     low = jnp.full((tiles, LANES), low_ref[0], jnp.int32).astype(jnp.float32) / 4.0
     high = jnp.full((tiles, LANES), high_ref[0], jnp.int32).astype(jnp.float32) / 4.0
     centre = (high + low) / 2.0
@@ -188,35 +193,30 @@
             dst_ref=sums.at[slot],
             send_sem=send_sems.at[d],
             recv_sem=recv_sems.at[slot],
-            device_id=coords(partner),
+            device_id=partner,
             device_id_type=MESH,
         )
 
-    def total_over(partial, sums, size, place, partners, send_sems, recv_sems):
-        sums[place] = partial
-        for d, partner in enumerate(partners):
-            spread_sums(sums, place, partner, send_sems, recv_sems, d).start()
-
-        def finish():
-            for d, partner in enumerate(partners):
-                slot = lax.rem(place + d + 1, size)
-                spread_sums(sums, slot, partner, send_sems, recv_sems, d).wait_recv()
-            total = sums[0]
-            for slot in range(1, size):
-                total = total + sums[slot]
-            return total
-
-        return finish
-
-    finish = total_over(partial, near_sums, near, near_me, near_partners, near_send, near_recv)
+    def slot_of(partner):
+        return partner[0] * aggs + partner[1] if one_round else partner[1]
+
+    near_sums[near_me] = partial
+    for d, partner in enumerate(near_partners):
+        spread_sums(near_sums, near_me, partner, near_send, near_recv, d).start()
     for j in range(comp):
         residual_out[pl.ds(j, tiles, stride=comp), :] = residual[j]
-    total = finish()
-    if far > 1:
-        total = total_over(total, far_sums, far, far_me, far_partners, far_send, far_recv)()
+    for d, partner in enumerate(near_partners):
+        spread_sums(near_sums, slot_of(partner), partner, near_send, near_recv, d).wait_recv()
+    total = jnp.sum(near_sums[...], axis=0)
+    if far_partners:
+        far_sums[sub] = total
+        for d, partner in enumerate(far_partners):
+            spread_sums(far_sums, sub, partner, far_send, far_recv, d).start()
+        for d, partner in enumerate(far_partners):
+            spread_sums(far_sums, partner[0], partner, far_send, far_recv, d).wait_recv()
+        total = jnp.sum(far_sums[...], axis=0)
     count = float(comp * rows * devices)
-    rms = jnp.sqrt(jnp.sum(total, axis=1, keepdims=True) / count + 1e-06)
-    rms_ref[0] = rms[0, 0]
+    rms_ref[...] = jnp.sqrt(jnp.sum(total, axis=1, keepdims=True) / count + 1e-06)
 
     for t in range(STEPS + 1):
         for way in range(2):
@@ -224,7 +224,19 @@
     for d, partner in enumerate(near_partners):
         spread_sums(near_sums, near_me, partner, near_send, near_recv, d).wait_send()
     for d, partner in enumerate(far_partners):
-        spread_sums(far_sums, far_me, partner, far_send, far_recv, d).wait_send()
+        spread_sums(far_sums, sub, partner, far_send, far_recv, d).wait_send()
+
+
+def put_out(*refs):
+    count = len(refs) // 2
+    sems = refs[-1]
+    copies = [
+        pltpu.make_async_copy(refs[i], refs[count + i], sems.at[i]) for i in range(count)
+    ]
+    for copy in copies:
+        copy.start()
+    for copy in copies:
+        copy.wait()
 
 
 def flat(field, tiles):
@@ -243,26 +255,23 @@
     blocks, comp, _, rows = block_values.shape
     tiles = rows // LANES
     devices = subs * aggs
-    near = group_size(devices)
-    far = devices // near
+    near, far = (devices, 1) if devices <= ONE_ROUND else (aggs, subs)
     f32 = jnp.float32
     plane = (tiles * comp, LANES)
+    anywhere = pl.BlockSpec(memory_space=pl.ANY)
     in_vmem = pl.BlockSpec(memory_space=pltpu.VMEM)
     in_hbm = pl.BlockSpec(memory_space=pltpu.HBM)
-    scalar = pl.BlockSpec(memory_space=pltpu.SMEM)
     dma = pltpu.SemaphoreType.DMA
     smoothed, residual, rms = pl.pallas_call(
         functools.partial(kernel, subs, aggs, (blocks, comp, tiles)),
         out_shape=(
             jax.ShapeDtypeStruct(plane, f32),
             jax.ShapeDtypeStruct(plane, f32),
-            jax.ShapeDtypeStruct((1,), f32),
+            jax.ShapeDtypeStruct((1, 1), f32),
         ),
-        in_specs=[in_hbm] * 6,
-        out_specs=(in_vmem, in_vmem, scalar),
+        in_specs=[in_hbm] * 4 + [pl.BlockSpec(memory_space=pltpu.SMEM)] * 2,
+        out_specs=(in_vmem,) * 3,
         scratch_shapes=[
-            pltpu.SMEM((1,), jnp.int32),
-            pltpu.SMEM((1,), jnp.int32),
             pltpu.VMEM((blocks * comp * comp * tiles, LANES), f32),
             pltpu.VMEM((blocks, rows), jnp.int32),
             pltpu.VMEM((8 * tiles, LANES), jnp.int32),
@@ -293,7 +302,19 @@
         ],
         bound_low, bound_high,
     )
-    return unflat(smoothed, comp), unflat(residual, comp), rms
+    smoothed, residual, rms = pl.pallas_call(
+        put_out,
+        out_shape=(
+            jax.ShapeDtypeStruct(plane, f32),
+            jax.ShapeDtypeStruct(plane, f32),
+            jax.ShapeDtypeStruct((1, 1), f32),
+        ),
+        in_specs=[anywhere] * 3,
+        out_specs=(anywhere,) * 3,
+        scratch_shapes=[dma((3,))],
+        compiler_params=pltpu.CompilerParams(vmem_limit_bytes=8 * 1024 * 1024),
+    )(smoothed, residual, rms)
+    return unflat(smoothed, comp), unflat(residual, comp), rms.reshape(1)
 
 
 def solution(mesh):

time: 38.7 us -> 37.3 us (0.964)
  between operations: 3.62 us -> 1.93 us
  Pallas kernels: 33.6 us -> 35.1 us
  local copies, waits for them, and re-layouts: 1.21 us -> 0 us
    pallas_call x0 -> x1, Pallas kernels: none -> 1.27 us  [shards(): pl.pallas_call(put_out, out_shape=(jax.ShapeDtypeStruct(plane, f32), jax....]
    unnamed x2 -> x0, local copies, waits for them, and re-layouts: 1.21 us -> none
where the time goes in v3:
time: 37.3 us; the launch traced here: 37.1 us
  Pallas kernels  35.1 us (94%)
  between operations  1.93 us (5%)
    pallas_call x1, Pallas kernels, shards(): pl.pallas_call(functools.partial(kernel, subs, aggs, (blocks, comp, tiles...  33.9 us
    pallas_call x1, Pallas kernels, shards(): pl.pallas_call(put_out, out_shape=(jax.ShapeDtypeStruct(plane, f32), jax....  1.27 us

profile of v3, /device:TPU:0, one launch (start us, length us, event | category | flops | bytes accessed | tf_op | source)
XLA Modules:
  0.0 37.1 jit_solution(9613253675432601830)
XLA Ops:
  1.9 33.9 %shard_map.85 = (f32[32,128]{1,0:T(8,128)S(1)}, f32[32,128]{1,0:T(8,128)S(1)}, f32[1,1]{1,0:T(1,128)}) custom-call(f32[896,128]{1,0:T(8,128)} %bitcast.26, s32[7,1024]{1,0:T(8,128)} %cols_hbm.1, f32[32,128]{1,0:T(8,128)} %bitcast.27, f32[32,128]{1,0:T(8,128)} %bitcast.28, s32[1]{0:T(128)S(6)} %copy.14.low_ref, s32[1]{0:T(128)S(6)} %copy.15.high_ref), custom_call_target="tpu_custom_call" | custom-call | tf_op jit(solution)/shard_map/pallas_call | solution.py:265
  35.8 1.3 %shard_map.86 = (f32[32,128]{1,0:T(8,128)}, f32[32,128]{1,0:T(8,128)}, f32[1,1]{1,0:T(1,128)}) custom-call(f32[32,128]{1,0:T(8,128)S(1)} %get-tuple-element.9.refs_0_, f32[32,128]{1,0:T(8,128)S(1)} %get-tuple-element.10.refs_1_, f32[1,1]{1,0:T(1,128)} %get-tuple-element.11.refs_2_), custom_call_target="tpu_custom_call" | custom-call | tf_op jit(solution)/shard_map/pallas_call | solution.py:305
